TPU v7x, 32 devices: a whole 2x2x4 slice. The times are simulated.
32 devices in a mesh: row: 4 (over z), col: 8 (over y, x, core).
Axes of the slice: x: 2, y: 2, z: 4, core: 2. Of those that a mesh axis runs over, the one named last changes fastest.
Arguments:
- right_side: float32 [256, 2048], P('row', 'col'), may hold values from -20 to 20
- initial_guess: float32 [256, 2048], P('row', 'col'), may hold values from -3 to 3
- kernel: float32 [31, 31], replicated, may hold values from 0 to 1, as said below
Outputs:
- template: float32 [256, 2048], P('row', 'col')
- residual: float32 [256, 2048], P('row', 'col')
Inputs may be any that keep to these rules, and one draw needn't show every extreme that they name: `kernel`: entries are positive and sum to one.
All inputs are finite; a program needn't handle non-finite values.
Results may differ from a plain program's by a relative error of at most 0.0003.
Values sent between devices are 32-bit elements; how exact they have to be, the bound alone decides.
A program may use at most 128 MiB of HBM per device.

v0:
```python
import math

import jax
import jax.numpy as jnp
from jax import lax
from jax.sharding import PartitionSpec as P

ITERS = 3


penalty = 0.05


def with_halo(x, sides, width):
    for axis, dim in sides:
        count, length = (lax.axis_size(axis), x.shape[dim])
        up = [(i, (i + 1) % count) for i in range(count - 1)]
        down = [(j, i) for i, j in up]
        last = lax.slice_in_dim(x, length - width, length, axis=dim)
        initial = lax.slice_in_dim(x, 0, width, axis=dim)
        before = lax.ppermute(last, axis, up)
        after = lax.ppermute(initial, axis, down)
        x = jnp.concatenate([before, x, after], axis=dim)
    return x


def banded_tables(taps, block_width):
    width = taps.shape[0]
    span = block_width + width - 1
    offset = (
        jnp.arange(span, dtype=jnp.int32)[:, None]
        - jnp.arange(block_width, dtype=jnp.int32)[None, :]
    )
    selector = (offset[None, :, :] == jnp.arange(width, dtype=jnp.int32)[:, None, None]).astype(
        jnp.float32
    )
    return jnp.einsum("ab,bkj->akj", taps, selector, precision=lax.Precision.HIGHEST)


def correlate(padded, taps):
    width = taps.shape[0]
    out_rows = padded.shape[0] - width + 1
    out_cols = padded.shape[1] - width + 1
    block_width = math.gcd(out_cols, 128)
    count = out_cols // block_width
    span = block_width + width - 1
    tables = banded_tables(taps, block_width)
    blocks = jnp.stack(
        [padded[:, index * block_width : index * block_width + span] for index in range(count)],
        axis=1,
    )
    total = jnp.zeros((out_rows, count, block_width), jnp.float32)
    for shift_row in range(width):
        window = blocks[shift_row : shift_row + out_rows]
        total = total + jnp.einsum(
            "rnk,kj->rnj", window, tables[shift_row], precision=lax.Precision.HIGHEST
        )
    return total.reshape(out_rows, out_cols)


def laplacian(padded, margin, tile_rows, tile_cols):
    center = padded[margin : margin + tile_rows, margin : margin + tile_cols]
    upper = padded[margin - 1 : margin - 1 + tile_rows, margin : margin + tile_cols]
    lower = padded[margin + 1 : margin + 1 + tile_rows, margin : margin + tile_cols]
    leftward = padded[margin : margin + tile_rows, margin - 1 : margin - 1 + tile_cols]
    rightward = padded[margin : margin + tile_rows, margin + 1 : margin + 1 + tile_cols]
    return 4.0 * center - upper - lower - leftward - rightward


def operate(source, kernel):
    tile_rows, tile_cols = source.shape
    half_width = kernel.shape[0] // 2
    flipped = kernel[::-1, ::-1]
    padded = with_halo(source, (("row", 0), ("col", 1)), half_width)
    blurred = correlate(padded, kernel)
    blurred_pad = with_halo(blurred, (("row", 0), ("col", 1)), half_width)
    back = correlate(blurred_pad, flipped)
    smooth_term = laplacian(padded, half_width, tile_rows, tile_cols)
    return back + penalty * smooth_term


def paired(residual, applied):
    return lax.psum((jnp.sum(residual * residual), jnp.sum(residual * applied)), ("row", "col"))


def on_device(right_side, initial_guess, kernel):
    template = initial_guess
    residual = right_side - operate(template, kernel)
    applied = operate(residual, kernel)
    norm_now, product = paired(residual, applied)
    step_size = norm_now / product
    direction, along = (residual, applied)
    for iteration in range(ITERS):
        template = template + step_size * direction
        residual = residual - step_size * along
        if iteration + 1 < ITERS:
            applied = operate(residual, kernel)
            norm_next, product = paired(residual, applied)
            ratio = norm_next / norm_now
            step_size = norm_next / (product - ratio * norm_next / step_size)
            direction = residual + ratio * direction
            along = applied + ratio * along
            norm_now = norm_next
    return (template, residual)


def solution(mesh):
    placed = (P("row", "col"), P("row", "col"), P())
    return jax.shard_map(
        on_device,
        mesh=mesh,
        in_specs=placed,
        out_specs=(P("row", "col"), P("row", "col")),
        check_vma=False,
    )
```

profile of v0, /device:TPU:0, one launch (start us, length us, event | category | flops | bytes accessed | tf_op | source)
XLA Modules:
  0.0 364.1 jit_solution(9057202369381304456)
XLA Ops:
  1.4 4.9 %collective-permute-start = (f32[15,256]{1,0:T(8,128)S(1)}, f32[15,256]{1,0:T(8,128)S(1)}, u32[]{:S(2)}, u32[]{:S(2)}) collective-permute-start(f32[15,256]{1,0:T(8,128)S(1)} %get-tuple-element.127), channel_id=1, source_target_pairs={{0,8},{8,16},{16,24},{1,9},{9,17},{17,25},{2,10},{10,18},{18,26},{... | collective-permute-start | bytes 46088 | tf_op jit(solution)/shard_map/ppermute | solution.py:21
  6.3 1.3 collective-permute-start.1
  8.4 2.0 fusion.2
  10.5 1.3 fusion.3
  11.8 1.3 fusion.1273
  13.2 1.3 fusion.1275
  14.7 1.3 collective-permute-start.3
  16.0 3.2 collective-permute-start.2
  28.8 1.3 collective-permute-start.5
  30.1 5.2 %collective-permute-start.4 = (f32[15,256]{1,0:T(8,128)S(1)}, f32[15,256]{1,0:T(8,128)S(1)}, u32[]{:S(2)}, u32[]{:S(2)}) collective-permute-start(f32[15,256]{1,0:T(8,128)S(1)} %bitcast.674), channel_id=1, source_target_pairs={{0,8},{8,16},{16,24},{1,9},{9,17},{17,25},{2,10},{10,18},{18,26},{... | collective-permute-start | bytes 46088 | tf_op jit(solution)/shard_map/ppermute | solution.py:21
  35.3 1.4 collective-permute-done.4
  36.8 1.3 collective-permute-start.7
  38.0 3.3 collective-permute-start.6
  50.9 4.2 %collective-permute-start.8 = (f32[15,256]{1,0:T(8,128)S(1)}, f32[15,256]{1,0:T(8,128)S(1)}, u32[]{:S(2)}, u32[]{:S(2)}) collective-permute-start(f32[15,256]{1,0:T(8,128)S(1)} %get-tuple-element.123), channel_id=1, source_target_pairs={{0,8},{8,16},{16,24},{1,9},{9,17},{17,25},{2,10},{10,18},{18,26},{... | collective-permute-start | bytes 46088 | tf_op jit(solution)/shard_map/ppermute | solution.py:21
  55.1 1.3 collective-permute-start.9
  56.5 4.3 %collective-permute-done.9 = f32[15,256]{1,0:T(8,128)S(1)} collective-permute-done((f32[15,256]{1,0:T(8,128)S(1)}, f32[15,256]{1,0:T(8,128)S(1)}, u32[]{:S(2)}, u32[]{:S(2)}) %collective-permute-start.9) | collective-permute-done | bytes 15392 | tf_op jit(solution)/shard_map/ppermute | solution.py:22
  60.9 3.7 %collective-permute-start.10 = (f32[94,15]{1,0:T(8,128)S(1)}, f32[94,15]{1,0:T(8,128)S(1)}, u32[]{:S(2)}, u32[]{:S(2)}) collective-permute-start(f32[94,15]{1,0:T(8,128)S(1)} %get-tuple-element.101), channel_id=1, source_target_pairs={{0,1},{1,2},{2,3},{3,4},{4,5},{5,6},{6,7},{8,9},{9,10},{10,11},{11... | collective-permute-start | bytes 16928 | tf_op jit(solution)/shard_map/ppermute | solution.py:21
  64.6 1.6 collective-permute-start.11
  66.2 4.5 %collective-permute-done.11 = f32[94,15]{1,0:T(8,128)S(1)} collective-permute-done((f32[94,15]{1,0:T(8,128)S(1)}, f32[94,15]{1,0:T(8,128)S(1)}, u32[]{:S(2)}, u32[]{:S(2)}) %collective-permute-start.11) | collective-permute-done | bytes 5672 | tf_op jit(solution)/shard_map/ppermute | solution.py:22
  79.5 1.3 collective-permute-start.13
  80.8 4.5 %collective-permute-start.12 = (f32[15,256]{1,0:T(8,128)S(1)}, f32[15,256]{1,0:T(8,128)S(1)}, u32[]{:S(2)}, u32[]{:S(2)}) collective-permute-start(f32[15,256]{1,0:T(8,128)S(1)} %bitcast.675), channel_id=1, source_target_pairs={{0,8},{8,16},{16,24},{1,9},{9,17},{17,25},{2,10},{10,18},{18,26},{... | collective-permute-start | bytes 46088 | tf_op jit(solution)/shard_map/ppermute | solution.py:21
  85.4 1.4 collective-permute-done.12
  86.9 1.3 collective-permute-start.15
  88.2 5.0 %collective-permute-start.14 = (f32[94,15]{1,0:T(8,128)S(1)}, f32[94,15]{1,0:T(8,128)S(1)}, u32[]{:S(2)}, u32[]{:S(2)}) collective-permute-start(f32[94,15]{1,0:T(8,128)S(1)} %get-tuple-element.98), channel_id=1, source_target_pairs={{0,1},{1,2},{2,3},{3,4},{4,5},{5,6},{6,7},{8,9},{9,10},{10,11},{11... | collective-permute-start | bytes 16928 | tf_op jit(solution)/shard_map/ppermute | solution.py:21
  103.0 47.4 %all-reduce.2 = (f32[]{:T(128)}, f32[]{:T(128)}) all-reduce(f32[]{:T(128)} %get-tuple-element.7, f32[]{:T(128)} %get-tuple-element.6), channel_id=1, replica_groups=mesh['row'=4,'col'=8] {'row','col'}, use_global_device_ids=true, to_apply=%region_1.0 | all-reduce | flops 2 | bytes 16 | tf_op jit(solution)/shard_map/psum | solution.py:83
  151.6 3.4 collective-permute-start.16
  155.0 1.3 collective-permute-start.17
  156.4 4.2 %collective-permute-done.17 = f32[15,256]{1,0:T(8,128)S(1)} collective-permute-done((f32[15,256]{1,0:T(8,128)S(1)}, f32[15,256]{1,0:T(8,128)S(1)}, u32[]{:S(2)}, u32[]{:S(2)}) %collective-permute-start.17) | collective-permute-done | bytes 15392 | tf_op jit(solution)/shard_map/ppermute | solution.py:22
  162.0 1.6 collective-permute-start.19
  163.6 4.2 %collective-permute-done.19 = f32[94,15]{1,0:T(8,128)S(1)} collective-permute-done((f32[94,15]{1,0:T(8,128)S(1)}, f32[94,15]{1,0:T(8,128)S(1)}, u32[]{:S(2)}, u32[]{:S(2)}) %collective-permute-start.19) | collective-permute-done | bytes 5672 | tf_op jit(solution)/shard_map/ppermute | solution.py:22
  184.6 1.3 collective-permute-start.21
  185.9 4.5 %collective-permute-start.20 = (f32[15,256]{1,0:T(8,128)S(1)}, f32[15,256]{1,0:T(8,128)S(1)}, u32[]{:S(2)}, u32[]{:S(2)}) collective-permute-start(f32[15,256]{1,0:T(8,128)S(1)} %bitcast.676), channel_id=1, source_target_pairs={{0,8},{8,16},{16,24},{1,9},{9,17},{17,25},{2,10},{10,18},{18,26},{... | collective-permute-start | bytes 46088 | tf_op jit(solution)/shard_map/ppermute | solution.py:21
  190.5 1.4 collective-permute-done.20
  191.9 1.3 collective-permute-start.23
  193.2 4.4 %collective-permute-start.22 = (f32[94,15]{1,0:T(8,128)S(1)}, f32[94,15]{1,0:T(8,128)S(1)}, u32[]{:S(2)}, u32[]{:S(2)}) collective-permute-start(f32[94,15]{1,0:T(8,128)S(1)} %get-tuple-element.90), channel_id=1, source_target_pairs={{0,1},{1,2},{2,3},{3,4},{4,5},{5,6},{6,7},{8,9},{9,10},{10,11},{11... | collective-permute-start | bytes 16928 | tf_op jit(solution)/shard_map/ppermute | solution.py:21
  206.9 1.4 multiply_reduce_fusion.2
  208.3 45.2 %all-reduce.1 = (f32[]{:T(128)}, f32[]{:T(128)}) all-reduce(f32[]{:T(128)} %get-tuple-element.5, f32[]{:T(128)} %get-tuple-element.4), channel_id=1, replica_groups=mesh['row'=4,'col'=8] {'row','col'}, use_global_device_ids=true, to_apply=%region_5.0 | all-reduce | flops 2 | bytes 16 | tf_op jit(solution)/shard_map/psum | solution.py:83
  258.8 2.5 collective-permute-start.24
  261.3 1.3 collective-permute-start.25
  262.7 4.2 %collective-permute-done.25 = f32[15,256]{1,0:T(8,128)S(1)} collective-permute-done((f32[15,256]{1,0:T(8,128)S(1)}, f32[15,256]{1,0:T(8,128)S(1)}, u32[]{:S(2)}, u32[]{:S(2)}) %collective-permute-start.25) | collective-permute-done | bytes 15392 | tf_op jit(solution)/shard_map/ppermute | solution.py:22
  268.3 1.7 collective-permute-start.27
  270.0 4.1 %collective-permute-done.27 = f32[94,15]{1,0:T(8,128)S(1)} collective-permute-done((f32[94,15]{1,0:T(8,128)S(1)}, f32[94,15]{1,0:T(8,128)S(1)}, u32[]{:S(2)}, u32[]{:S(2)}) %collective-permute-start.27) | collective-permute-done | bytes 5672 | tf_op jit(solution)/shard_map/ppermute | solution.py:22
  290.9 1.3 collective-permute-start.29
  292.2 4.5 %collective-permute-start.28 = (f32[15,256]{1,0:T(8,128)S(1)}, f32[15,256]{1,0:T(8,128)S(1)}, u32[]{:S(2)}, u32[]{:S(2)}) collective-permute-start(f32[15,256]{1,0:T(8,128)S(1)} %bitcast.673), channel_id=1, source_target_pairs={{0,8},{8,16},{16,24},{1,9},{9,17},{17,25},{2,10},{10,18},{18,26},{... | collective-permute-start | bytes 46088 | tf_op jit(solution)/shard_map/ppermute | solution.py:21
  296.8 1.4 collective-permute-done.28
  298.3 1.3 collective-permute-start.31
  299.6 4.5 %collective-permute-start.30 = (f32[94,15]{1,0:T(8,128)S(1)}, f32[94,15]{1,0:T(8,128)S(1)}, u32[]{:S(2)}, u32[]{:S(2)}) collective-permute-start(f32[94,15]{1,0:T(8,128)S(1)} %get-tuple-element.82), channel_id=1, source_target_pairs={{0,1},{1,2},{2,3},{3,4},{4,5},{5,6},{6,7},{8,9},{9,10},{10,11},{11... | collective-permute-start | bytes 16928 | tf_op jit(solution)/shard_map/ppermute | solution.py:21
  314.0 45.1 %all-reduce = (f32[]{:T(128)}, f32[]{:T(128)}) all-reduce(f32[]{:T(128)} %get-tuple-element.3, f32[]{:T(128)} %get-tuple-element.2), channel_id=1, replica_groups=mesh['row'=4,'col'=8] {'row','col'}, use_global_device_ids=true, to_apply=%region_9.0 | all-reduce | flops 2 | bytes 16 | tf_op jit(solution)/shard_map/psum | solution.py:83
  (451 shorter events, 94.5 us)
Async XLA Ops:
  1.4 13.2 %collective-permute-start = (f32[15,256]{1,0:T(8,128)S(1)}, f32[15,256]{1,0:T(8,128)S(1)}, u32[]{:S(2)}, u32[]{:S(2)}) collective-permute-start(f32[15,256]{1,0:T(8,128)S(1)} %get-tuple-element.127), channel_id=1, source_target_pairs={{0,8},{8,16},{16,24},{1,9},{9,17},{17,25},{2,10},{10,18},{18,26},{... | collective-permute-start | bytes 46088 | tf_op jit(solution)/shard_map/ppermute | solution.py:21
  6.3 8.2 %collective-permute-start.1 = (f32[15,256]{1,0:T(8,128)S(1)}, f32[15,256]{1,0:T(8,128)S(1)}, u32[]{:S(2)}, u32[]{:S(2)}) collective-permute-start(f32[15,256]{1,0:T(8,128)S(1)} %get-tuple-element.128), channel_id=1, source_target_pairs={{8,0},{16,8},{24,16},{9,1},{17,9},{25,17},{10,2},{18,10},{26,18},{... | collective-permute-start | bytes 46088 | tf_op jit(solution)/shard_map/ppermute | solution.py:22
  14.7 5.4 %collective-permute-start.3 = (f32[94,15]{1,0:T(8,128)S(1)}, f32[94,15]{1,0:T(8,128)S(1)}, u32[]{:S(2)}, u32[]{:S(2)}) collective-permute-start(f32[94,15]{1,0:T(8,128)S(1)} %get-tuple-element.109), channel_id=1, source_target_pairs={{1,0},{2,1},{3,2},{4,3},{5,4},{6,5},{7,6},{9,8},{10,9},{11,10},{12... | collective-permute-start | bytes 16928 | tf_op jit(solution)/shard_map/ppermute | solution.py:22
  16.0 4.1 %collective-permute-start.2 = (f32[94,15]{1,0:T(8,128)S(1)}, f32[94,15]{1,0:T(8,128)S(1)}, u32[]{:S(2)}, u32[]{:S(2)}) collective-permute-start(f32[94,15]{1,0:T(8,128)S(1)} %get-tuple-element.110), channel_id=1, source_target_pairs={{0,1},{1,2},{2,3},{3,4},{4,5},{5,6},{6,7},{8,9},{9,10},{10,11},{11... | collective-permute-start | bytes 16928 | tf_op jit(solution)/shard_map/ppermute | solution.py:21
  20.0 52.6 %copy-start.38 = (f32[1,158,128]{2,0,1:T(1,128)}, f32[1,158,128]{2,0,1:T(1,128)S(1)}, u32[]{:S(2)}) copy-start(f32[1,158,128]{2,0,1:T(1,128)S(1)} %get-tuple-element.72) | copy-start | bytes 242692
  20.0 52.9 %copy-start.37 = (f32[1,158,128]{2,0,1:T(1,128)}, f32[1,158,128]{2,0,1:T(1,128)S(1)}, u32[]{:S(2)}) copy-start(f32[1,158,128]{2,0,1:T(1,128)S(1)} %get-tuple-element.71) | copy-start | bytes 242692
  20.0 53.2 %copy-start.33 = (f32[1,158,128]{2,0,1:T(1,128)}, f32[1,158,128]{2,0,1:T(1,128)S(1)}, u32[]{:S(2)}) copy-start(f32[1,158,128]{2,0,1:T(1,128)S(1)} %get-tuple-element.70) | copy-start | bytes 242692
  20.0 53.4 %copy-start.27 = (f32[1,158,128]{2,0,1:T(1,128)}, f32[1,158,128]{2,0,1:T(1,128)S(1)}, u32[]{:S(2)}) copy-start(f32[1,158,128]{2,0,1:T(1,128)S(1)} %get-tuple-element.69) | copy-start | bytes 242692
  20.1 53.7 %copy-start.21 = (f32[1,158,128]{2,0,1:T(1,128)}, f32[1,158,128]{2,0,1:T(1,128)S(1)}, u32[]{:S(2)}) copy-start(f32[1,158,128]{2,0,1:T(1,128)S(1)} %get-tuple-element.68) | copy-start | bytes 242692
  20.1 54.0 %copy-start.15 = (f32[1,158,128]{2,0,1:T(1,128)}, f32[1,158,128]{2,0,1:T(1,128)S(1)}, u32[]{:S(2)}) copy-start(f32[1,158,128]{2,0,1:T(1,128)S(1)} %get-tuple-element.67) | copy-start | bytes 242692
  28.8 6.5 %collective-permute-start.5 = (f32[15,256]{1,0:T(8,128)S(1)}, f32[15,256]{1,0:T(8,128)S(1)}, u32[]{:S(2)}, u32[]{:S(2)}) collective-permute-start(f32[15,256]{1,0:T(8,128)S(1)} %bitcast.677), channel_id=1, source_target_pairs={{8,0},{16,8},{24,16},{9,1},{17,9},{25,17},{10,2},{18,10},{26,18},{... | collective-permute-start | bytes 46088 | tf_op jit(solution)/shard_map/ppermute | solution.py:22
  30.1 6.6 %collective-permute-start.4 = (f32[15,256]{1,0:T(8,128)S(1)}, f32[15,256]{1,0:T(8,128)S(1)}, u32[]{:S(2)}, u32[]{:S(2)}) collective-permute-start(f32[15,256]{1,0:T(8,128)S(1)} %bitcast.674), channel_id=1, source_target_pairs={{0,8},{8,16},{16,24},{1,9},{9,17},{17,25},{2,10},{10,18},{18,26},{... | collective-permute-start | bytes 46088 | tf_op jit(solution)/shard_map/ppermute | solution.py:21
  36.8 5.4 %collective-permute-start.7 = (f32[94,15]{1,0:T(8,128)S(1)}, f32[94,15]{1,0:T(8,128)S(1)}, u32[]{:S(2)}, u32[]{:S(2)}) collective-permute-start(f32[94,15]{1,0:T(8,128)S(1)} %get-tuple-element.105), channel_id=1, source_target_pairs={{1,0},{2,1},{3,2},{4,3},{5,4},{6,5},{7,6},{9,8},{10,9},{11,10},{12... | collective-permute-start | bytes 16928 | tf_op jit(solution)/shard_map/ppermute | solution.py:22
  38.0 4.1 %collective-permute-start.6 = (f32[94,15]{1,0:T(8,128)S(1)}, f32[94,15]{1,0:T(8,128)S(1)}, u32[]{:S(2)}, u32[]{:S(2)}) collective-permute-start(f32[94,15]{1,0:T(8,128)S(1)} %get-tuple-element.106), channel_id=1, source_target_pairs={{0,1},{1,2},{2,3},{3,4},{4,5},{5,6},{6,7},{8,9},{9,10},{10,11},{11... | collective-permute-start | bytes 16928 | tf_op jit(solution)/shard_map/ppermute | solution.py:21
  42.1 52.4 %copy-start.18 = (f32[1,158,128]{2,0,1:T(1,128)}, f32[1,158,128]{2,0,1:T(1,128)S(1)}, u32[]{:S(2)}) copy-start(f32[1,158,128]{2,0,1:T(1,128)S(1)} %get-tuple-element.44) | copy-start | bytes 242692
  42.1 52.7 %copy-start.12 = (f32[1,158,128]{2,0,1:T(1,128)}, f32[1,158,128]{2,0,1:T(1,128)S(1)}, u32[]{:S(2)}) copy-start(f32[1,158,128]{2,0,1:T(1,128)S(1)} %get-tuple-element.43) | copy-start | bytes 242692
  42.1 53.0 %copy-start.9 = (f32[1,158,128]{2,0,1:T(1,128)}, f32[1,158,128]{2,0,1:T(1,128)S(1)}, u32[]{:S(2)}) copy-start(f32[1,158,128]{2,0,1:T(1,128)S(1)} %get-tuple-element.42) | copy-start | bytes 242692
  42.1 53.2 %copy-start.6 = (f32[1,158,128]{2,0,1:T(1,128)}, f32[1,158,128]{2,0,1:T(1,128)S(1)}, u32[]{:S(2)}) copy-start(f32[1,158,128]{2,0,1:T(1,128)S(1)} %get-tuple-element.41) | copy-start | bytes 242692
  42.1 53.5 %copy-start.3 = (f32[1,158,128]{2,0,1:T(1,128)}, f32[1,158,128]{2,0,1:T(1,128)S(1)}, u32[]{:S(2)}) copy-start(f32[1,158,128]{2,0,1:T(1,128)S(1)} %get-tuple-element.40) | copy-start | bytes 242692
  42.2 53.8 %copy-start = (f32[1,158,128]{2,0,1:T(1,128)}, f32[1,158,128]{2,0,1:T(1,128)S(1)}, u32[]{:S(2)}) copy-start(f32[1,158,128]{2,0,1:T(1,128)S(1)} %get-tuple-element.39) | copy-start | bytes 242692
  50.9 5.6 %collective-permute-start.8 = (f32[15,256]{1,0:T(8,128)S(1)}, f32[15,256]{1,0:T(8,128)S(1)}, u32[]{:S(2)}, u32[]{:S(2)}) collective-permute-start(f32[15,256]{1,0:T(8,128)S(1)} %get-tuple-element.123), channel_id=1, source_target_pairs={{0,8},{8,16},{16,24},{1,9},{9,17},{17,25},{2,10},{10,18},{18,26},{... | collective-permute-start | bytes 46088 | tf_op jit(solution)/shard_map/ppermute | solution.py:21
  55.1 5.7 %collective-permute-start.9 = (f32[15,256]{1,0:T(8,128)S(1)}, f32[15,256]{1,0:T(8,128)S(1)}, u32[]{:S(2)}, u32[]{:S(2)}) collective-permute-start(f32[15,256]{1,0:T(8,128)S(1)} %get-tuple-element.124), channel_id=1, source_target_pairs={{8,0},{16,8},{24,16},{9,1},{17,9},{25,17},{10,2},{18,10},{26,18},{... | collective-permute-start | bytes 46088 | tf_op jit(solution)/shard_map/ppermute | solution.py:22
  60.9 5.3 %collective-permute-start.10 = (f32[94,15]{1,0:T(8,128)S(1)}, f32[94,15]{1,0:T(8,128)S(1)}, u32[]{:S(2)}, u32[]{:S(2)}) collective-permute-start(f32[94,15]{1,0:T(8,128)S(1)} %get-tuple-element.101), channel_id=1, source_target_pairs={{0,1},{1,2},{2,3},{3,4},{4,5},{5,6},{6,7},{8,9},{9,10},{10,11},{11... | collective-permute-start | bytes 16928 | tf_op jit(solution)/shard_map/ppermute | solution.py:21
  64.6 6.1 %collective-permute-start.11 = (f32[94,15]{1,0:T(8,128)S(1)}, f32[94,15]{1,0:T(8,128)S(1)}, u32[]{:S(2)}, u32[]{:S(2)}) collective-permute-start(f32[94,15]{1,0:T(8,128)S(1)} %get-tuple-element.102), channel_id=1, source_target_pairs={{1,0},{2,1},{3,2},{4,3},{5,4},{6,5},{7,6},{9,8},{10,9},{11,10},{12... | collective-permute-start | bytes 16928 | tf_op jit(solution)/shard_map/ppermute | solution.py:22
  79.5 5.9 %collective-permute-start.13 = (f32[15,256]{1,0:T(8,128)S(1)}, f32[15,256]{1,0:T(8,128)S(1)}, u32[]{:S(2)}, u32[]{:S(2)}) collective-permute-start(f32[15,256]{1,0:T(8,128)S(1)} %bitcast.678), channel_id=1, source_target_pairs={{8,0},{16,8},{24,16},{9,1},{17,9},{25,17},{10,2},{18,10},{26,18},{... | collective-permute-start | bytes 46088 | tf_op jit(solution)/shard_map/ppermute | solution.py:22
  80.8 6.0 %collective-permute-start.12 = (f32[15,256]{1,0:T(8,128)S(1)}, f32[15,256]{1,0:T(8,128)S(1)}, u32[]{:S(2)}, u32[]{:S(2)}) collective-permute-start(f32[15,256]{1,0:T(8,128)S(1)} %bitcast.675), channel_id=1, source_target_pairs={{0,8},{8,16},{16,24},{1,9},{9,17},{17,25},{2,10},{10,18},{18,26},{... | collective-permute-start | bytes 46088 | tf_op jit(solution)/shard_map/ppermute | solution.py:21
  86.9 6.3 %collective-permute-start.15 = (f32[94,15]{1,0:T(8,128)S(1)}, f32[94,15]{1,0:T(8,128)S(1)}, u32[]{:S(2)}, u32[]{:S(2)}) collective-permute-start(f32[94,15]{1,0:T(8,128)S(1)} %get-tuple-element.97), channel_id=1, source_target_pairs={{1,0},{2,1},{3,2},{4,3},{5,4},{6,5},{7,6},{9,8},{10,9},{11,10},{12... | collective-permute-start | bytes 16928 | tf_op jit(solution)/shard_map/ppermute | solution.py:22
  88.2 5.4 %collective-permute-start.14 = (f32[94,15]{1,0:T(8,128)S(1)}, f32[94,15]{1,0:T(8,128)S(1)}, u32[]{:S(2)}, u32[]{:S(2)}) collective-permute-start(f32[94,15]{1,0:T(8,128)S(1)} %get-tuple-element.98), channel_id=1, source_target_pairs={{0,1},{1,2},{2,3},{3,4},{4,5},{5,6},{6,7},{8,9},{9,10},{10,11},{11... | collective-permute-start | bytes 16928 | tf_op jit(solution)/shard_map/ppermute | solution.py:21
  103.0 75.4 %copy-start.47 = (f32[64,256]{1,0:T(8,128)}, f32[64,256]{1,0:T(8,128)S(1)}, u32[]{:S(2)}) copy-start(f32[64,256]{1,0:T(8,128)S(1)} %get-tuple-element.16) | copy-start | bytes 196612
  151.6 4.8 %collective-permute-start.16 = (f32[15,256]{1,0:T(8,128)S(1)}, f32[15,256]{1,0:T(8,128)S(1)}, u32[]{:S(2)}, u32[]{:S(2)}) collective-permute-start(f32[15,256]{1,0:T(8,128)S(1)} %get-tuple-element.119), channel_id=1, source_target_pairs={{0,8},{8,16},{16,24},{1,9},{9,17},{17,25},{2,10},{10,18},{18,26},{... | collective-permute-start | bytes 46088 | tf_op jit(solution)/shard_map/ppermute | solution.py:21
  155.0 5.6 %collective-permute-start.17 = (f32[15,256]{1,0:T(8,128)S(1)}, f32[15,256]{1,0:T(8,128)S(1)}, u32[]{:S(2)}, u32[]{:S(2)}) collective-permute-start(f32[15,256]{1,0:T(8,128)S(1)} %get-tuple-element.120), channel_id=1, source_target_pairs={{8,0},{16,8},{24,16},{9,1},{17,9},{25,17},{10,2},{18,10},{26,18},{... | collective-permute-start | bytes 46088 | tf_op jit(solution)/shard_map/ppermute | solution.py:22
  160.7 2.9 collective-permute-start.18
  162.0 5.8 %collective-permute-start.19 = (f32[94,15]{1,0:T(8,128)S(1)}, f32[94,15]{1,0:T(8,128)S(1)}, u32[]{:S(2)}, u32[]{:S(2)}) collective-permute-start(f32[94,15]{1,0:T(8,128)S(1)} %get-tuple-element.94), channel_id=1, source_target_pairs={{1,0},{2,1},{3,2},{4,3},{5,4},{6,5},{7,6},{9,8},{10,9},{11,10},{12... | collective-permute-start | bytes 16928 | tf_op jit(solution)/shard_map/ppermute | solution.py:22
  184.6 5.9 %collective-permute-start.21 = (f32[15,256]{1,0:T(8,128)S(1)}, f32[15,256]{1,0:T(8,128)S(1)}, u32[]{:S(2)}, u32[]{:S(2)}) collective-permute-start(f32[15,256]{1,0:T(8,128)S(1)} %bitcast.679), channel_id=1, source_target_pairs={{8,0},{16,8},{24,16},{9,1},{17,9},{25,17},{10,2},{18,10},{26,18},{... | collective-permute-start | bytes 46088 | tf_op jit(solution)/shard_map/ppermute | solution.py:22
  185.9 6.0 %collective-permute-start.20 = (f32[15,256]{1,0:T(8,128)S(1)}, f32[15,256]{1,0:T(8,128)S(1)}, u32[]{:S(2)}, u32[]{:S(2)}) collective-permute-start(f32[15,256]{1,0:T(8,128)S(1)} %bitcast.676), channel_id=1, source_target_pairs={{0,8},{8,16},{16,24},{1,9},{9,17},{17,25},{2,10},{10,18},{18,26},{... | collective-permute-start | bytes 46088 | tf_op jit(solution)/shard_map/ppermute | solution.py:21
  191.9 5.7 %collective-permute-start.23 = (f32[94,15]{1,0:T(8,128)S(1)}, f32[94,15]{1,0:T(8,128)S(1)}, u32[]{:S(2)}, u32[]{:S(2)}) collective-permute-start(f32[94,15]{1,0:T(8,128)S(1)} %get-tuple-element.89), channel_id=1, source_target_pairs={{1,0},{2,1},{3,2},{4,3},{5,4},{6,5},{7,6},{9,8},{10,9},{11,10},{12... | collective-permute-start | bytes 16928 | tf_op jit(solution)/shard_map/ppermute | solution.py:22
  193.2 5.1 %collective-permute-start.22 = (f32[94,15]{1,0:T(8,128)S(1)}, f32[94,15]{1,0:T(8,128)S(1)}, u32[]{:S(2)}, u32[]{:S(2)}) collective-permute-start(f32[94,15]{1,0:T(8,128)S(1)} %get-tuple-element.90), channel_id=1, source_target_pairs={{0,1},{1,2},{2,3},{3,4},{4,5},{5,6},{6,7},{8,9},{9,10},{10,11},{11... | collective-permute-start | bytes 16928 | tf_op jit(solution)/shard_map/ppermute | solution.py:21
  258.8 3.9 %collective-permute-start.24 = (f32[15,256]{1,0:T(8,128)S(1)}, f32[15,256]{1,0:T(8,128)S(1)}, u32[]{:S(2)}, u32[]{:S(2)}) collective-permute-start(f32[15,256]{1,0:T(8,128)S(1)} %get-tuple-element.115), channel_id=1, source_target_pairs={{0,8},{8,16},{16,24},{1,9},{9,17},{17,25},{2,10},{10,18},{18,26},{... | collective-permute-start | bytes 46088 | tf_op jit(solution)/shard_map/ppermute | solution.py:21
  261.3 5.6 %collective-permute-start.25 = (f32[15,256]{1,0:T(8,128)S(1)}, f32[15,256]{1,0:T(8,128)S(1)}, u32[]{:S(2)}, u32[]{:S(2)}) collective-permute-start(f32[15,256]{1,0:T(8,128)S(1)} %get-tuple-element.116), channel_id=1, source_target_pairs={{8,0},{16,8},{24,16},{9,1},{17,9},{25,17},{10,2},{18,10},{26,18},{... | collective-permute-start | bytes 46088 | tf_op jit(solution)/shard_map/ppermute | solution.py:22
  267.0 3.0 collective-permute-start.26
  268.3 5.8 %collective-permute-start.27 = (f32[94,15]{1,0:T(8,128)S(1)}, f32[94,15]{1,0:T(8,128)S(1)}, u32[]{:S(2)}, u32[]{:S(2)}) collective-permute-start(f32[94,15]{1,0:T(8,128)S(1)} %get-tuple-element.86), channel_id=1, source_target_pairs={{1,0},{2,1},{3,2},{4,3},{5,4},{6,5},{7,6},{9,8},{10,9},{11,10},{12... | collective-permute-start | bytes 16928 | tf_op jit(solution)/shard_map/ppermute | solution.py:22
  290.9 5.9 %collective-permute-start.29 = (f32[15,256]{1,0:T(8,128)S(1)}, f32[15,256]{1,0:T(8,128)S(1)}, u32[]{:S(2)}, u32[]{:S(2)}) collective-permute-start(f32[15,256]{1,0:T(8,128)S(1)} %bitcast.680), channel_id=1, source_target_pairs={{8,0},{16,8},{24,16},{9,1},{17,9},{25,17},{10,2},{18,10},{26,18},{... | collective-permute-start | bytes 46088 | tf_op jit(solution)/shard_map/ppermute | solution.py:22
  292.2 6.0 %collective-permute-start.28 = (f32[15,256]{1,0:T(8,128)S(1)}, f32[15,256]{1,0:T(8,128)S(1)}, u32[]{:S(2)}, u32[]{:S(2)}) collective-permute-start(f32[15,256]{1,0:T(8,128)S(1)} %bitcast.673), channel_id=1, source_target_pairs={{0,8},{8,16},{16,24},{1,9},{9,17},{17,25},{2,10},{10,18},{18,26},{... | collective-permute-start | bytes 46088 | tf_op jit(solution)/shard_map/ppermute | solution.py:21
  298.3 5.8 %collective-permute-start.31 = (f32[94,15]{1,0:T(8,128)S(1)}, f32[94,15]{1,0:T(8,128)S(1)}, u32[]{:S(2)}, u32[]{:S(2)}) collective-permute-start(f32[94,15]{1,0:T(8,128)S(1)} %get-tuple-element.81), channel_id=1, source_target_pairs={{1,0},{2,1},{3,2},{4,3},{5,4},{6,5},{7,6},{9,8},{10,9},{11,10},{12... | collective-permute-start | bytes 16928 | tf_op jit(solution)/shard_map/ppermute | solution.py:22
  299.6 5.1 %collective-permute-start.30 = (f32[94,15]{1,0:T(8,128)S(1)}, f32[94,15]{1,0:T(8,128)S(1)}, u32[]{:S(2)}, u32[]{:S(2)}) collective-permute-start(f32[94,15]{1,0:T(8,128)S(1)} %get-tuple-element.82), channel_id=1, source_target_pairs={{0,1},{1,2},{2,3},{3,4},{4,5},{5,6},{6,7},{8,9},{9,10},{10,11},{11... | collective-permute-start | bytes 16928 | tf_op jit(solution)/shard_map/ppermute | solution.py:21
  310.0 53.1 %copy-start.46 = (f32[64,256]{1,0:T(8,128)S(1)}, f32[64,256]{1,0:T(8,128)}, u32[]{:S(2)}) copy-start(f32[64,256]{1,0:T(8,128)} %param.4) | copy-start | bytes 196612
  310.0 53.1 %copy-start.48 = (f32[64,256]{1,0:T(8,128)S(1)}, f32[64,256]{1,0:T(8,128)}, u32[]{:S(2)}) copy-start(f32[64,256]{1,0:T(8,128)} %copy-done.47) | copy-start | bytes 196612
  310.0 53.1 %copy-start.49 = (f32[64,256]{1,0:T(8,128)S(1)}, f32[64,256]{1,0:T(8,128)}, u32[]{:S(2)}) copy-start(f32[64,256]{1,0:T(8,128)} %get-tuple-element.15) | copy-start | bytes 196612
  (35 other events, 897.7 us)
where the time goes:
time: 370 us; the launch traced here: 364 us
  blocking collectives  138 us (37%)
  matrix products  84.5 us (23%)
  starting transfers between devices  82.1 us (22%)
  waiting for transfers between devices  33 us (9%)
  between operations  13.8 us (4%)
  local copies, waits for them, and re-layouts  7.13 us (2%)
  other arithmetic  5.84 us (2%)
    psum x3, blocking collectives, paired(): lax.psum((jnp.sum(residual * residual), jnp.sum(residual * applied)), ('r...  138 us
    dot_general x248, matrix products, correlate(): jnp.einsum('rnk,kj->rnj', window, tables[shift_row], precision=lax.Precis...  81.2 us
    ppermute x16, starting transfers between devices, with_halo(): before = lax.ppermute(last, axis, up)  60.5 us
    ppermute x16, waiting for transfers between devices, with_halo(): after = lax.ppermute(initial, axis, down)  25.5 us
    ppermute x16, starting transfers between devices, with_halo(): after = lax.ppermute(initial, axis, down)  21.6 us
    ppermute x16, waiting for transfers between devices, with_halo(): before = lax.ppermute(last, axis, up)  7.52 us
  transfers between devices with their start and end apart: 32, of which 16 were waited for; matrix products, arithmetic and copies ran while one was open for 2% of the time, Pallas kernels for 0%

commit v1 on v0

v1 whole, which is shorter than its diff:
```python
import functools

import jax
import jax.numpy as jnp
from jax import lax
from jax.experimental import pallas as pl
from jax.experimental.pallas import tpu as pltpu
from jax.sharding import PartitionSpec as P

ITERS = 3
PENALTY = 0.05
EDGE_ROWS = 16
EDGE_COLS = 128
GROUP = 8
MESH = pl.DeviceIdType.MESH
DIRECTIONS = ((-1, -1), (-1, 1), (1, -1), (1, 1), (-1, 0), (1, 0), (0, -1), (0, 1))


def span(step, size, edge):
    if step > 0:
        return size, 0, edge
    if step < 0:
        return edge, size + edge, edge
    return edge, edge, size


def split(x):
    high = x.astype(jnp.bfloat16)
    low = (x - high.astype(jnp.float32)).astype(jnp.bfloat16)
    return high, low


def body(
    n_row, n_col, half,
    right_ref, guess_ref, base_ref, template_ref, residual_ref,
    ext, tables, red, send_sem, recv_sem, red_send, red_recv,
):
    rows, cols = right_ref.shape
    row, col = lax.axis_index("row"), lax.axis_index("col")
    me, count = row * n_col + col, n_row * n_col
    tall, wide = rows + 2 * EDGE_ROWS, cols + 2 * EDGE_COLS
    groups = tables.shape[1]
    mid_r, mid_c = pl.ds(EDGE_ROWS, rows), pl.ds(EDGE_COLS, cols)

    barrier = pltpu.get_barrier_semaphore()

    def greet(step, carry):
        other = lax.rem(me + step, count)
        pl.semaphore_signal(
            barrier, inc=1, device_id=(other // n_col, lax.rem(other, n_col)), device_id_type=MESH
        )
        return carry

    lax.fori_loop(1, count, greet, 0)

    phases = ext.shape[0]
    ext[0, mid_r, mid_c] = guess_ref[...]

    @pl.when(row == 0)
    def _():
        ext[:, 0:EDGE_ROWS, :] = jnp.zeros((phases, EDGE_ROWS, wide), jnp.float32)

    @pl.when(row == n_row - 1)
    def _():
        ext[:, EDGE_ROWS + rows : tall, :] = jnp.zeros((phases, EDGE_ROWS, wide), jnp.float32)

    @pl.when(col == 0)
    def _():
        ext[:, :, 0:EDGE_COLS] = jnp.zeros((phases, tall, EDGE_COLS), jnp.float32)

    @pl.when(col == n_col - 1)
    def _():
        ext[:, :, EDGE_COLS + cols : wide] = jnp.zeros((phases, tall, EDGE_COLS), jnp.float32)

    def inside(dr, dc):
        checks = []
        if dr:
            checks.append(row + dr >= 0 if dr < 0 else row + dr < n_row)
        if dc:
            checks.append(col + dc >= 0 if dc < 0 else col + dc < n_col)
        return functools.reduce(jnp.logical_and, checks)

    def strip(phase, index):
        dr, dc = DIRECTIONS[index]
        r_src, r_dst, r_len = span(dr, rows, EDGE_ROWS)
        c_src, c_dst, c_len = span(dc, cols, EDGE_COLS)
        return pltpu.make_async_remote_copy(
            src_ref=ext.at[phase, pl.ds(r_src, r_len), pl.ds(c_src, c_len)],
            dst_ref=ext.at[phase, pl.ds(r_dst, r_len), pl.ds(c_dst, c_len)],
            send_sem=send_sem.at[phase, index],
            recv_sem=recv_sem.at[phase, index],
            device_id=(row + dr, col + dc),
            device_id_type=MESH,
        )

    def send(phase):
        for index, (dr, dc) in enumerate(DIRECTIONS):
            pl.when(inside(dr, dc))(lambda index=index: strip(phase, index).start())

    def receive(phase):
        for index, (dr, dc) in enumerate(DIRECTIONS):
            pl.when(inside(-dr, -dc))(lambda index=index: strip(phase, index).wait_recv())

    def finish(phase):
        for index, (dr, dc) in enumerate(DIRECTIONS):
            pl.when(inside(dr, dc))(lambda index=index: strip(phase, index).wait_send())

    sub = lax.broadcasted_iota(jnp.int32, (8, base_ref.shape[2]), 0)

    def build(which):
        for group in range(groups):
            line = base_ref[which, group : group + 1, :]
            eight = pltpu.roll(
                jnp.broadcast_to(line, (8, line.shape[1])), EDGE_ROWS - half, axis=1
            )
            for bit in (1, 2, 4):
                eight = jnp.where((sub & bit) != 0, pltpu.roll(eight, bit, axis=1), eight)
            blocks = [eight if k == 0 else pltpu.roll(eight, 8 * k, axis=1) for k in range(rows // 8)]
            high, low = split(jnp.concatenate(blocks, axis=0))
            tables[which, group, 0:rows, :] = high
            tables[which, group, rows : 2 * rows, :] = low

    def correlate(phase, which):
        both = jnp.zeros((2 * rows, cols), jnp.float32)
        rest = jnp.zeros((rows, cols), jnp.float32)
        whole = ext[phase]
        for group in range(groups):
            highs, lows = [], []
            for k in range(GROUP):
                offset = EDGE_COLS - half + group * GROUP + k
                high, low = split(pltpu.roll(whole, wide - offset, axis=1)[:, 0:cols])
                highs.append(high)
                lows.append(low)
            table = tables[which, group]
            both = both + jnp.dot(
                table, jnp.concatenate(highs, axis=0), preferred_element_type=jnp.float32
            )
            rest = rest + jnp.dot(
                table[0:rows], jnp.concatenate(lows, axis=0), preferred_element_type=jnp.float32
            )
        return both[0:rows] + (both[rows:] + rest)

    def laplacian(phase):
        center = ext[phase, mid_r, mid_c]
        upper = ext[phase, pl.ds(EDGE_ROWS - 1, rows), mid_c]
        lower = ext[phase, pl.ds(EDGE_ROWS + 1, rows), mid_c]
        band = ext[phase, mid_r, :]
        left = pltpu.roll(band, 1, axis=1)[:, EDGE_COLS : EDGE_COLS + cols]
        right = pltpu.roll(band, wide - 1, axis=1)[:, EDGE_COLS : EDGE_COLS + cols]
        return 4.0 * center - upper - lower - left - right

    def operate(phase):
        receive(phase)
        ext[phase + 1, mid_r, mid_c] = correlate(phase, 0)
        send(phase + 1)
        smooth = PENALTY * laplacian(phase)
        receive(phase + 1)
        return correlate(phase + 1, 1) + smooth

    def put(phase, value):
        ext[phase, mid_r, mid_c] = value
        send(phase)

    lane = lax.broadcasted_iota(jnp.int32, (1, 128), 1)

    def fold(x):
        line = jnp.sum(x, axis=0, keepdims=True)
        line = functools.reduce(
            jnp.add, [line[:, k : k + 128] for k in range(0, line.shape[1], 128)]
        )
        return line + pltpu.roll(line, 64, axis=1)

    def spread(slot, residual, applied):
        red[slot, me] = jnp.where(lane < 64, fold(residual * residual), fold(residual * applied))

        def one(step, carry):
            other = lax.rem(me + step, count)
            pltpu.make_async_remote_copy(
                src_ref=red.at[slot, me],
                dst_ref=red.at[slot, me],
                send_sem=red_send.at[slot],
                recv_sem=red_recv.at[slot],
                device_id=(other // n_col, lax.rem(other, n_col)),
                device_id_type=MESH,
            ).start()
            return carry

        lax.fori_loop(1, count, one, 0)

    def all_slots(slot):
        return pltpu.make_async_remote_copy(
            src_ref=red.at[slot, pl.ds(0, count - 1)],
            dst_ref=red.at[slot, pl.ds(0, count - 1)],
            send_sem=red_send.at[slot],
            recv_sem=red_recv.at[slot],
            device_id=(row, col),
            device_id_type=MESH,
        )

    def gather(slot):
        all_slots(slot).wait_recv()
        line = jnp.sum(red[slot], axis=0)
        norm = jnp.sum(jnp.where(lane < 64, line, 0.0), axis=1, keepdims=True)
        product = jnp.sum(jnp.where(lane < 64, 0.0, line), axis=1, keepdims=True)
        return norm, product

    pl.semaphore_wait(barrier, count - 1)
    send(0)
    build(0)
    build(1)

    template = guess_ref[...]
    residual = right_ref[...] - operate(0)
    put(2, residual)
    applied = operate(2)
    norm_last = step_size = None
    direction = along = beyond = None
    for iteration in range(ITERS):
        last = iteration + 1 == ITERS
        if not last:
            put(4 + 2 * iteration, applied)
        spread(iteration, residual, applied)
        twice = None if last else operate(4 + 2 * iteration)
        norm, product = gather(iteration)
        if iteration == 0:
            step_size = norm / product
            direction, along, beyond = residual, applied, twice
        else:
            ratio = norm / norm_last
            step_size = norm / (product - ratio * norm / step_size)
            direction = residual + ratio * direction
            along = applied + ratio * along
            if not last:
                beyond = twice + ratio * beyond
        norm_last = norm
        template = template + step_size * direction
        residual = residual - step_size * along
        if not last:
            applied = applied - step_size * beyond

    template_ref[...] = template
    residual_ref[...] = residual
    for phase in range(phases):
        finish(phase)
    for slot in range(ITERS):
        all_slots(slot).wait_send()


def on_device(n_row, n_col, right_side, initial_guess, kernel):
    rows, cols = right_side.shape
    width = kernel.shape[0]
    tall = rows + 2 * EDGE_ROWS
    groups = -(-width // GROUP)
    both = jnp.stack([kernel.T, kernel[::-1, ::-1].T])
    base = jnp.pad(both, ((0, 0), (0, groups * GROUP - width), (0, tall - width)))
    base = base.reshape(2, groups, GROUP * tall)
    phases, count = 2 * (ITERS + 1), n_row * n_col
    shape = jax.ShapeDtypeStruct((rows, cols), jnp.float32)
    vmem = pl.BlockSpec(memory_space=pltpu.VMEM)
    return pl.pallas_call(
        functools.partial(body, n_row, n_col, width // 2),
        out_shape=(shape, shape),
        in_specs=[vmem] * 3,
        out_specs=(vmem, vmem),
        scratch_shapes=[
            pltpu.VMEM((phases, tall, cols + 2 * EDGE_COLS), jnp.float32),
            pltpu.VMEM((2, groups, 2 * rows, GROUP * tall), jnp.bfloat16),
            pltpu.VMEM((ITERS, count, 1, 128), jnp.float32),
            pltpu.SemaphoreType.DMA((phases, len(DIRECTIONS))),
            pltpu.SemaphoreType.DMA((phases, len(DIRECTIONS))),
            pltpu.SemaphoreType.DMA((ITERS,)),
            pltpu.SemaphoreType.DMA((ITERS,)),
        ],
        compiler_params=pltpu.CompilerParams(collective_id=0, has_side_effects=True),
    )(right_side, initial_guess, base)


def solution(mesh):
    placed = (P("row", "col"), P("row", "col"), P())
    return jax.shard_map(
        functools.partial(on_device, mesh.shape["row"], mesh.shape["col"]),
        mesh=mesh,
        in_specs=placed,
        out_specs=(P("row", "col"), P("row", "col")),
        check_vma=False,
    )
```

time: 370 us -> 56.8 us (0.15); the launches traced: 364 us -> 56.5 us
  blocking collectives: 138 us -> 0 us
  matrix products: 84.5 us -> 0 us
  starting transfers between devices: 82.1 us -> 0 us
  Pallas kernels: 0 us -> 52.1 us
  waiting for transfers between devices: 33 us -> 0 us
  between operations: 13.8 us -> 0.66 us
  other arithmetic: 5.84 us -> 0.01 us
    psum x3 -> x0, blocking collectives: 138 us -> none  [paired(): lax.psum((jnp.sum(residual * residual), jnp.sum(residual * applied)), ('r...]
    dot_general x250 -> x0, matrix products: 84.5 us -> none  [the longest x248 81.2 us: correlate(): jnp.einsum('rnk,kj->rnj', window, tables[shift_row], precision=lax.Precis...]
    ppermute x32 -> x0, starting transfers between devices: 82.1 us -> none  [the longest x16 60.5 us: with_halo(): before = lax.ppermute(last, axis, up)]
    pallas_call x0 -> x1, Pallas kernels: none -> 52.1 us  [on_device(): pl.pallas_call(functools.partial(body, n_row, n_col, width // 2), out_sha...]
    ppermute x32 -> x0, waiting for transfers between devices: 33 us -> none  [the longest x16 25.5 us: with_halo(): after = lax.ppermute(initial, axis, down)]
    slice x28 -> x0, local copies, waits for them, and re-layouts: 5.63 us -> none  [the longest x4 4.15 us: correlate(): tables[shift_row]]
  transfers between devices with their start and end apart: 32 -> 0, of which waited for: 16 -> 0; matrix products, arithmetic and copies ran while one was open for 2% -> 0% of each run, Pallas kernels for 0% -> 0%
where the time goes in v1:
time: 56.8 us; the launch traced here: 56.5 us
  Pallas kernels  52.1 us (92%)
  local copies, waits for them, and re-layouts  3.81 us (7%)
  between operations  0.66 us (1%)
    pallas_call x1, Pallas kernels, on_device(): pl.pallas_call(functools.partial(body, n_row, n_col, width // 2), out_sha...  52.1 us
    unnamed x7, local copies, waits for them, and re-layouts  2.24 us

profile of v1, /device:TPU:0, one launch (start us, length us, event | category | flops | bytes accessed | tf_op | source)
XLA Modules:
  0.0 56.5 jit_solution(10307581924711987698)
XLA Ops:
  0.6 0.0 copy-start.1
  0.6 0.9 %rev.3 = f32[31,31]{1,0:T(8,128)S(1)} reverse(f32[31,31]{1,0:T(8,128)} %param.5), dimensions={0,1} | reverse | bytes 7688 | tf_op jit(solution)/shard_map/rev | solution.py:254
  1.5 0.0 copy-done.1
  1.5 0.1 copy.6
  1.6 0.7 %reshape.7.base_ref = f32[2,4,768]{2,1,0:T(4,128)} reshape(f32[2,32,96]{2,1,0:T(8,128)S(1)} %pad.4.clone) | data formatting | bytes 49152 | tf_op jit(solution)/shard_map/reshape | solution.py:256
  2.3 52.1 %shard_map.50 = (f32[64,256]{1,0:T(8,128)}, f32[64,256]{1,0:T(8,128)}) custom-call(f32[64,256]{1,0:T(8,128)} %right_ref.1, f32[64,256]{1,0:T(8,128)} %guess_ref.1, f32[2,4,768]{2,1,0:T(4,128)} %reshape.7.base_ref), custom_call_target="tpu_custom_call" | custom-call | tf_op jit(solution)/shard_map/pallas_call | solution.py:260
  54.4 0.0 copy-start
  54.4 1.5 %copy.9 = f32[64,256]{1,0:T(8,128)} copy(f32[64,256]{1,0:T(8,128)} %get-tuple-element.4) | data formatting | bytes 131072
  55.9 0.0 copy-done
  55.9 0.6 %copy.10 = f32[64,256]{1,0:T(8,128)} copy(f32[64,256]{1,0:T(8,128)S(1)} %copy-done) | data formatting | bytes 131072
  (2 shorter events, 0.0 us)
Async XLA Ops:
  0.6 0.9 %copy-start.1 = (f32[31,31]{1,0:T(8,128)S(1)}, f32[31,31]{1,0:T(8,128)}, u32[]{:S(2)}) copy-start(f32[31,31]{1,0:T(8,128)} %param.5) | copy-start | bytes 11536
  54.4 1.5 %copy-start = (f32[64,256]{1,0:T(8,128)S(1)}, f32[64,256]{1,0:T(8,128)}, u32[]{:S(2)}) copy-start(f32[64,256]{1,0:T(8,128)} %get-tuple-element.5) | copy-start | bytes 196612

commit v2 on v1

v2 whole, which is shorter than its diff:
```python
import functools

import jax
import jax.numpy as jnp
from jax import lax
from jax.experimental import pallas as pl
from jax.experimental.pallas import tpu as pltpu
from jax.sharding import PartitionSpec as P

ITERS = 3
PENALTY = 0.05
EDGE_ROWS = 16
EDGE_COLS = 128
DEPTH = 512
LANES = 128
MESH = pl.DeviceIdType.MESH
DIRECTIONS = ((-1, -1), (-1, 1), (1, -1), (1, 1), (0, -1), (0, 1), (-1, 0), (1, 0))
SIDES = (4, 5)
OTHERS = (0, 1, 2, 3, 6, 7)


def span(step, size, edge):
    if step > 0:
        return size, 0, edge
    if step < 0:
        return edge, size + edge, edge
    return edge, edge, size


def split(x):
    high = x.astype(jnp.bfloat16)
    low = (x - high.astype(jnp.float32)).astype(jnp.bfloat16)
    return high, low


def body(
    n_row, n_col,
    right_ref, guess_ref, kernel_ref, template_ref, residual_ref,
    ext, mid_table, edge_table, red, send_sem, recv_sem, red_send, red_recv,
):
    rows, cols = right_ref.shape
    row, col = lax.axis_index("row"), lax.axis_index("col")
    me, count = row * n_col + col, n_row * n_col
    tall, wide = rows + 2 * EDGE_ROWS, cols + 2 * EDGE_COLS
    width = kernel_ref.shape[0]
    half = width // 2
    shifts = mid_table.shape[2] // rows
    mid_r, mid_c = pl.ds(EDGE_ROWS, rows), pl.ds(EDGE_COLS, cols)

    barrier = pltpu.get_barrier_semaphore()

    def others(act):
        def along_row(r, carry):
            def one(c, inner):
                pl.when(r * n_col + c != me)(lambda: act((r, c)))
                return inner

            return lax.fori_loop(0, n_col, one, carry)

        lax.fori_loop(0, n_row, along_row, 0)

    others(
        lambda place: pl.semaphore_signal(barrier, inc=1, device_id=place, device_id_type=MESH)
    )

    phases = ext.shape[0]
    ext[0, mid_r, mid_c] = guess_ref[...]

    @pl.when(row == 0)
    def _():
        ext[:, 0:EDGE_ROWS, :] = jnp.zeros((phases, EDGE_ROWS, wide), jnp.float32)

    @pl.when(row == n_row - 1)
    def _():
        ext[:, EDGE_ROWS + rows : tall, :] = jnp.zeros((phases, EDGE_ROWS, wide), jnp.float32)

    @pl.when(col == 0)
    def _():
        ext[:, :, 0:EDGE_COLS] = jnp.zeros((phases, tall, EDGE_COLS), jnp.float32)

    @pl.when(col == n_col - 1)
    def _():
        ext[:, :, EDGE_COLS + cols : wide] = jnp.zeros((phases, tall, EDGE_COLS), jnp.float32)

    def inside(dr, dc):
        checks = []
        if dr:
            checks.append(row + dr >= 0 if dr < 0 else row + dr < n_row)
        if dc:
            checks.append(col + dc >= 0 if dc < 0 else col + dc < n_col)
        return functools.reduce(jnp.logical_and, checks)

    def strip(phase, index):
        dr, dc = DIRECTIONS[index]
        r_src, r_dst, r_len = span(dr, rows, EDGE_ROWS)
        c_src, c_dst, c_len = span(dc, cols, EDGE_COLS)
        return pltpu.make_async_remote_copy(
            src_ref=ext.at[phase, pl.ds(r_src, r_len), pl.ds(c_src, c_len)],
            dst_ref=ext.at[phase, pl.ds(r_dst, r_len), pl.ds(c_dst, c_len)],
            send_sem=send_sem.at[phase, index],
            recv_sem=recv_sem.at[phase, index],
            device_id=(row + dr, col + dc),
            device_id_type=MESH,
        )

    def send(phase):
        for index, (dr, dc) in enumerate(DIRECTIONS):
            pl.when(inside(dr, dc))(lambda index=index: strip(phase, index).start())

    def receive(phase, which):
        for index in which:
            dr, dc = DIRECTIONS[index]
            pl.when(inside(-dr, -dc))(lambda index=index: strip(phase, index).wait_recv())

    def finish(phase):
        for index, (dr, dc) in enumerate(DIRECTIONS):
            pl.when(inside(dr, dc))(lambda index=index: strip(phase, index).wait_send())

    sub = lax.broadcasted_iota(jnp.int32, (8, LANES), 0)
    lane8 = lax.broadcasted_iota(jnp.int32, (8, LANES), 1)
    per_mid, edge_span = LANES // rows, 2 * EDGE_ROWS
    per_edge = LANES // edge_span

    def build(which):
        taps = kernel_ref[...]
        if which:
            taps = jnp.concatenate([taps[a : a + 1] for a in reversed(range(width))], axis=0)
        taps = jnp.concatenate([taps, jnp.zeros((LANES - width, width), jnp.float32)], axis=0)
        taps = jnp.concatenate([taps, jnp.zeros((LANES, LANES - width), jnp.float32)], axis=1)
        taps = taps.T
        bands = []
        for b in range(shifts):
            if b >= width:
                bands.append(None)
                continue
            source = width - 1 - b if which else b
            eight = pltpu.roll(
                jnp.broadcast_to(taps[source : source + 1, :], (8, LANES)), EDGE_ROWS - half, axis=1
            )
            for bit in (1, 2, 4):
                eight = jnp.where((sub & bit) != 0, pltpu.roll(eight, bit, axis=1), eight)
            bands.append(eight)

        def moved(b, k, shift):
            if bands[b] is None:
                return jnp.zeros((8, LANES), jnp.float32)
            return pltpu.roll(bands[b], (8 * k + shift) % LANES, axis=1)

        def keep(table, tile, blocks):
            high, low = split(jnp.concatenate(blocks, axis=0))
            table[which, 0:rows, tile * LANES : (tile + 1) * LANES] = high
            table[which, rows : 2 * rows, tile * LANES : (tile + 1) * LANES] = low

        for tile in range(shifts // per_mid):
            blocks = []
            for k in range(rows // 8):
                block = moved(tile * per_mid, k, -EDGE_ROWS)
                for q in range(1, per_mid):
                    block = jnp.where(
                        lane8 < q * rows,
                        block,
                        moved(tile * per_mid + q, k, q * rows - EDGE_ROWS),
                    )
                blocks.append(block)
            keep(mid_table, tile, blocks)
        for tile in range(shifts // per_edge):
            blocks = []
            for k in range(rows // 8):
                block = None
                for q in range(per_edge):
                    b, start = tile * per_edge + q, q * edge_span
                    upper = moved(b, k, start)
                    lower = moved(b, k, start - rows)
                    piece = jnp.where(lane8 < start + EDGE_ROWS, upper, lower)
                    block = piece if block is None else jnp.where(lane8 < start, block, piece)
                blocks.append(block)
            keep(edge_table, tile, blocks)

    def part(source, table, which):
        depth = source.shape[0]
        group = DEPTH // depth
        both = jnp.zeros((2 * rows, cols), jnp.float32)
        rest = jnp.zeros((rows, cols), jnp.float32)
        for first in range(0, shifts, group):
            highs, lows = [], []
            for b in range(first, first + group):
                offset = EDGE_COLS - half + min(b, width - 1)
                high, low = split(pltpu.roll(source, wide - offset, axis=1)[:, 0:cols])
                highs.append(high)
                lows.append(low)
            block = table[which, :, first * depth : (first + group) * depth]
            both = both + jnp.dot(
                block, jnp.concatenate(highs, axis=0), preferred_element_type=jnp.float32
            )
            rest = rest + jnp.dot(
                block[0:rows], jnp.concatenate(lows, axis=0), preferred_element_type=jnp.float32
            )
        return both[0:rows] + (both[rows:] + rest)

    def correlate(phase, which):
        receive(phase, SIDES)
        middle = part(ext[phase, mid_r, :], mid_table, which)
        receive(phase, OTHERS)
        edges = jnp.concatenate(
            [ext[phase, 0:EDGE_ROWS, :], ext[phase, EDGE_ROWS + rows : tall, :]], axis=0
        )
        return middle + part(edges, edge_table, which)

    def laplacian(phase):
        center = ext[phase, mid_r, mid_c]
        upper = ext[phase, pl.ds(EDGE_ROWS - 1, rows), mid_c]
        lower = ext[phase, pl.ds(EDGE_ROWS + 1, rows), mid_c]
        band = ext[phase, mid_r, :]
        left = pltpu.roll(band, 1, axis=1)[:, EDGE_COLS : EDGE_COLS + cols]
        right = pltpu.roll(band, wide - 1, axis=1)[:, EDGE_COLS : EDGE_COLS + cols]
        return 4.0 * center - upper - lower - left - right

    def operate(phase, slot=None):
        blurred = correlate(phase, 0)
        put(phase + 1, blurred)
        smooth = PENALTY * laplacian(phase)
        if slot is not None:
            center = ext[phase, mid_r, mid_c]
            spread(slot, center * center, blurred * blurred + center * smooth)
        return correlate(phase + 1, 1) + smooth

    def put(phase, value):
        ext[phase, mid_r, mid_c] = value
        send(phase)

    lane = lane8[0:1]

    def fold(x):
        line = jnp.sum(x, axis=0, keepdims=True)
        line = functools.reduce(
            jnp.add, [line[:, k : k + 128] for k in range(0, line.shape[1], 128)]
        )
        return line + pltpu.roll(line, 64, axis=1)

    def spread(slot, norms, products):
        red[slot, me] = jnp.where(lane < 64, fold(norms), fold(products))
        others(
            lambda place: pltpu.make_async_remote_copy(
                src_ref=red.at[slot, me],
                dst_ref=red.at[slot, me],
                send_sem=red_send.at[slot],
                recv_sem=red_recv.at[slot],
                device_id=place,
                device_id_type=MESH,
            ).start()
        )

    def all_slots(slot):
        return pltpu.make_async_remote_copy(
            src_ref=red.at[slot, pl.ds(0, count - 1)],
            dst_ref=red.at[slot, pl.ds(0, count - 1)],
            send_sem=red_send.at[slot],
            recv_sem=red_recv.at[slot],
            device_id=(row, col),
            device_id_type=MESH,
        )

    def gather(slot):
        all_slots(slot).wait_recv()
        line = jnp.sum(red[slot], axis=0)
        norm = jnp.sum(jnp.where(lane < 64, line, 0.0), axis=1, keepdims=True)
        product = jnp.sum(jnp.where(lane < 64, 0.0, line), axis=1, keepdims=True)
        return norm, product

    pl.semaphore_wait(barrier, count - 1)
    send(0)
    build(0)
    build(1)

    template = guess_ref[...]
    residual = right_ref[...] - operate(0)
    norm_last = step_size = direction = along = None
    for iteration in range(ITERS):
        put(2 * iteration + 2, residual)
        applied = operate(2 * iteration + 2, iteration)
        norm, product = gather(iteration)
        if iteration == 0:
            step_size = norm / product
            direction, along = residual, applied
        else:
            ratio = norm / norm_last
            step_size = norm / (product - ratio * norm / step_size)
            direction = residual + ratio * direction
            along = applied + ratio * along
        norm_last = norm
        template = template + step_size * direction
        residual = residual - step_size * along

    template_ref[...] = template
    residual_ref[...] = residual
    for phase in range(phases):
        finish(phase)
    for slot in range(ITERS):
        all_slots(slot).wait_send()


def on_device(n_row, n_col, right_side, initial_guess, kernel):
    rows, cols = right_side.shape
    tall = rows + 2 * EDGE_ROWS
    group = DEPTH // (2 * EDGE_ROWS)
    shifts = -(-kernel.shape[0] // group) * group
    phases, count = 2 * (ITERS + 1), n_row * n_col
    shape = jax.ShapeDtypeStruct((rows, cols), jnp.float32)
    vmem = pl.BlockSpec(memory_space=pltpu.VMEM)
    return pl.pallas_call(
        functools.partial(body, n_row, n_col),
        out_shape=(shape, shape),
        in_specs=[vmem] * 3,
        out_specs=(vmem, vmem),
        scratch_shapes=[
            pltpu.VMEM((phases, tall, cols + 2 * EDGE_COLS), jnp.float32),
            pltpu.VMEM((2, 2 * rows, shifts * rows), jnp.bfloat16),
            pltpu.VMEM((2, 2 * rows, shifts * 2 * EDGE_ROWS), jnp.bfloat16),
            pltpu.VMEM((ITERS, count, 1, 128), jnp.float32),
            pltpu.SemaphoreType.DMA((phases, len(DIRECTIONS))),
            pltpu.SemaphoreType.DMA((phases, len(DIRECTIONS))),
            pltpu.SemaphoreType.DMA((ITERS,)),
            pltpu.SemaphoreType.DMA((ITERS,)),
        ],
        compiler_params=pltpu.CompilerParams(collective_id=0, has_side_effects=True),
    )(right_side, initial_guess, kernel)


def solution(mesh):
    placed = (P("row", "col"), P("row", "col"), P())
    return jax.shard_map(
        functools.partial(on_device, mesh.shape["row"], mesh.shape["col"]),
        mesh=mesh,
        in_specs=placed,
        out_specs=(P("row", "col"), P("row", "col")),
        check_vma=False,
    )
```

time: 56.8 us -> 53.5 us (0.942)
  local copies, waits for them, and re-layouts: 3.81 us -> 2.14 us
  Pallas kernels: 52.1 us -> 50.5 us
    pallas_call x1, Pallas kernels: 52.1 us -> 50.5 us  [on_device(): pl.pallas_call(functools.partial(body, n_row, n_col), out_shape=(shape, s...]
    rev x1 -> x0, local copies, waits for them, and re-layouts: 0.86 us -> none  [on_device(): both = jnp.stack([kernel.T, kernel[::-1, ::-1].T])]
    reshape x1 -> x0, local copies, waits for them, and re-layouts: 0.7 us -> none  [on_device(): base = base.reshape(2, groups, GROUP * tall)]
    unnamed x7 -> x4, local copies, waits for them, and re-layouts: 2.24 us -> 2.14 us
where the time goes in v2:
time: 53.5 us; the launch traced here: 53.3 us
  Pallas kernels  50.5 us (94%)
  local copies, waits for them, and re-layouts  2.14 us (4%)
  between operations  0.65 us (1%)
    pallas_call x1, Pallas kernels, on_device(): pl.pallas_call(functools.partial(body, n_row, n_col), out_shape=(shape, s...  50.5 us
    unnamed x4, local copies, waits for them, and re-layouts  2.14 us

profile of v2, /device:TPU:0, one launch (start us, length us, event | category | flops | bytes accessed | tf_op | source)
XLA Modules:
  0.0 53.3 jit_solution(6463532305002048314)
XLA Ops:
  0.6 50.5 %shard_map.50 = (f32[64,256]{1,0:T(8,128)}, f32[64,256]{1,0:T(8,128)}) custom-call(f32[64,256]{1,0:T(8,128)} %right_ref.1, f32[64,256]{1,0:T(8,128)} %guess_ref.1, f32[31,31]{1,0:T(8,128)} %kernel_ref.1), custom_call_target="tpu_custom_call" | custom-call | tf_op jit(solution)/shard_map/pallas_call | solution.py:310
  51.1 0.0 copy-start
  51.1 1.5 %copy.7 = f32[64,256]{1,0:T(8,128)} copy(f32[64,256]{1,0:T(8,128)} %get-tuple-element.4) | data formatting | bytes 131072
  52.7 0.0 copy-done
  52.7 0.6 %copy.8 = f32[64,256]{1,0:T(8,128)} copy(f32[64,256]{1,0:T(8,128)S(1)} %copy-done) | data formatting | bytes 131072
Async XLA Ops:
  51.1 1.5 %copy-start = (f32[64,256]{1,0:T(8,128)S(1)}, f32[64,256]{1,0:T(8,128)}, u32[]{:S(2)}) copy-start(f32[64,256]{1,0:T(8,128)} %get-tuple-element.5) | copy-start | bytes 196612

commit v3 on v2

--- a/solution.py
+++ b/solution.py
@@ -36,7 +36,8 @@
 def body(
     n_row, n_col,
     right_ref, guess_ref, kernel_ref, template_ref, residual_ref,
-    ext, mid_table, edge_table, red, send_sem, recv_sem, red_send, red_recv,
+    ext, taps_ref, mid_table, edge_table, got, smooth_ref, along_ref, direction_ref, last_ref,
+    red, send_sem, recv_sem, red_send, red_recv,
 ):
     rows, cols = right_ref.shape
     row, col = lax.axis_index("row"), lax.axis_index("col")
@@ -44,7 +45,7 @@
     tall, wide = rows + 2 * EDGE_ROWS, cols + 2 * EDGE_COLS
     width = kernel_ref.shape[0]
     half = width // 2
-    shifts = mid_table.shape[2] // rows
+    shifts = mid_table.shape[1] * LANES // rows
     mid_r, mid_c = pl.ds(EDGE_ROWS, rows), pl.ds(EDGE_COLS, cols)
 
     barrier = pltpu.get_barrier_semaphore()
@@ -121,60 +122,60 @@
     per_mid, edge_span = LANES // rows, 2 * EDGE_ROWS
     per_edge = LANES // edge_span
 
-    def build(which):
+    def flip(x):
+        return jnp.concatenate([x[a : a + 1] for a in reversed(range(width))] + [x[width:]], axis=0)
+
+    def prepare():
         taps = kernel_ref[...]
-        if which:
-            taps = jnp.concatenate([taps[a : a + 1] for a in reversed(range(width))], axis=0)
-        taps = jnp.concatenate([taps, jnp.zeros((LANES - width, width), jnp.float32)], axis=0)
-        taps = jnp.concatenate([taps, jnp.zeros((LANES, LANES - width), jnp.float32)], axis=1)
-        taps = taps.T
+        taps = jnp.concatenate([taps, jnp.zeros((width, LANES - width), jnp.float32)], axis=1)
+        taps = jnp.concatenate([taps, jnp.zeros((LANES - width, LANES), jnp.float32)], axis=0)
+        taps_ref[0] = taps.T
+        taps_ref[1] = flip(flip(taps).T)
+
+    def build(which, quad):
         bands = []
-        for b in range(shifts):
-            if b >= width:
-                bands.append(None)
-                continue
-            source = width - 1 - b if which else b
-            eight = pltpu.roll(
-                jnp.broadcast_to(taps[source : source + 1, :], (8, LANES)), EDGE_ROWS - half, axis=1
-            )
+        for q in range(per_edge):
+            line = taps_ref[which, pl.ds(quad * per_edge + q, 1), :]
+            eight = pltpu.roll(jnp.broadcast_to(line, (8, LANES)), EDGE_ROWS - half, axis=1)
             for bit in (1, 2, 4):
                 eight = jnp.where((sub & bit) != 0, pltpu.roll(eight, bit, axis=1), eight)
             bands.append(eight)
 
-        def moved(b, k, shift):
-            if bands[b] is None:
-                return jnp.zeros((8, LANES), jnp.float32)
-            return pltpu.roll(bands[b], (8 * k + shift) % LANES, axis=1)
+        def moved(q, k, shift):
+            return pltpu.roll(bands[q], (8 * k + shift) % LANES, axis=1)
 
         def keep(table, tile, blocks):
             high, low = split(jnp.concatenate(blocks, axis=0))
-            table[which, 0:rows, tile * LANES : (tile + 1) * LANES] = high
-            table[which, rows : 2 * rows, tile * LANES : (tile + 1) * LANES] = low
-
-        for tile in range(shifts // per_mid):
+            table[which, tile, 0:rows, :] = high
+            table[which, tile, rows : 2 * rows, :] = low
+
+        for t in range(per_edge // per_mid):
             blocks = []
             for k in range(rows // 8):
-                block = moved(tile * per_mid, k, -EDGE_ROWS)
+                block = moved(t * per_mid, k, -EDGE_ROWS)
                 for q in range(1, per_mid):
-                    block = jnp.where(
-                        lane8 < q * rows,
-                        block,
-                        moved(tile * per_mid + q, k, q * rows - EDGE_ROWS),
-                    )
+                    other = moved(t * per_mid + q, k, q * rows - EDGE_ROWS)
+                    block = jnp.where(lane8 < q * rows, block, other)
                 blocks.append(block)
-            keep(mid_table, tile, blocks)
-        for tile in range(shifts // per_edge):
-            blocks = []
-            for k in range(rows // 8):
-                block = None
-                for q in range(per_edge):
-                    b, start = tile * per_edge + q, q * edge_span
-                    upper = moved(b, k, start)
-                    lower = moved(b, k, start - rows)
-                    piece = jnp.where(lane8 < start + EDGE_ROWS, upper, lower)
-                    block = piece if block is None else jnp.where(lane8 < start, block, piece)
-                blocks.append(block)
-            keep(edge_table, tile, blocks)
+            keep(mid_table, quad * (per_edge // per_mid) + t, blocks)
+        blocks = []
+        for k in range(rows // 8):
+            block = None
+            for q in range(per_edge):
+                start = q * edge_span
+                upper = moved(q, k, start)
+                lower = moved(q, k, start - rows)
+                piece = jnp.where(lane8 < start + EDGE_ROWS, upper, lower)
+                block = piece if block is None else jnp.where(lane8 < start, block, piece)
+            blocks.append(block)
+        keep(edge_table, quad, blocks)
+
+    def build_half(which):
+        def inner(quad, c):
+            build(which, quad)
+            return c
+
+        lax.fori_loop(0, shifts // per_edge, inner, 0)
 
     def part(source, table, which):
         depth = source.shape[0]
@@ -188,7 +189,8 @@
                 high, low = split(pltpu.roll(source, wide - offset, axis=1)[:, 0:cols])
                 highs.append(high)
                 lows.append(low)
-            block = table[which, :, first * depth : (first + group) * depth]
+            tiles = range(first * depth // LANES, (first + group) * depth // LANES)
+            block = jnp.concatenate([table[which, t] for t in tiles], axis=1)
             both = both + jnp.dot(
                 block, jnp.concatenate(highs, axis=0), preferred_element_type=jnp.float32
             )
@@ -214,15 +216,6 @@
         left = pltpu.roll(band, 1, axis=1)[:, EDGE_COLS : EDGE_COLS + cols]
         right = pltpu.roll(band, wide - 1, axis=1)[:, EDGE_COLS : EDGE_COLS + cols]
         return 4.0 * center - upper - lower - left - right
-
-    def operate(phase, slot=None):
-        blurred = correlate(phase, 0)
-        put(phase + 1, blurred)
-        smooth = PENALTY * laplacian(phase)
-        if slot is not None:
-            center = ext[phase, mid_r, mid_c]
-            spread(slot, center * center, blurred * blurred + center * smooth)
-        return correlate(phase + 1, 1) + smooth
 
     def put(phase, value):
         ext[phase, mid_r, mid_c] = value
@@ -267,36 +260,68 @@
         product = jnp.sum(jnp.where(lane < 64, 0.0, line), axis=1, keepdims=True)
         return norm, product
 
+    template_ref[...] = guess_ref[...]
+    along_ref[...] = jnp.zeros_like(along_ref)
+    direction_ref[...] = jnp.zeros_like(direction_ref)
+    last_ref[...] = jnp.ones_like(last_ref)
+    prepare()
+    build_half(0)
     pl.semaphore_wait(barrier, count - 1)
     send(0)
-    build(0)
-    build(1)
-
-    template = guess_ref[...]
-    residual = right_ref[...] - operate(0)
-    norm_last = step_size = direction = along = None
-    for iteration in range(ITERS):
-        put(2 * iteration + 2, residual)
-        applied = operate(2 * iteration + 2, iteration)
-        norm, product = gather(iteration)
-        if iteration == 0:
-            step_size = norm / product
-            direction, along = residual, applied
-        else:
-            ratio = norm / norm_last
-            step_size = norm / (product - ratio * norm / step_size)
-            direction = residual + ratio * direction
-            along = applied + ratio * along
-        norm_last = norm
-        template = template + step_size * direction
-        residual = residual - step_size * along
-
-    template_ref[...] = template
-    residual_ref[...] = residual
-    for phase in range(phases):
+    build_half(1)
+
+    def update(slot):
+        applied = got[...] + smooth_ref[...]
+        residual = residual_ref[...]
+        norm, product = gather(slot)
+        norm_last, step_last = last_ref[0:1, 0:1], last_ref[1:2, 0:1]
+        ratio = jnp.where(slot > 0, norm / norm_last, 0.0)
+        step_size = norm / (product - ratio * norm / step_last)
+        direction = residual + ratio * direction_ref[...]
+        along = applied + ratio * along_ref[...]
+        direction_ref[...], along_ref[...] = direction, along
+        last_ref[0:1, :] = jnp.broadcast_to(norm, (1, LANES))
+        last_ref[1:2, :] = jnp.broadcast_to(step_size, (1, LANES))
+        template_ref[...] = template_ref[...] + step_size * direction
+        residual_ref[...] = residual - step_size * along
+
+    def advance(phase, carry):
+        which, slot = lax.rem(phase, 2), phase // 2 - 1
+        got[...] = correlate(phase, which)
+
+        @pl.when(which == 0)
+        def _():
+            put(phase + 1, got[...])
+            smooth = PENALTY * laplacian(phase)
+            smooth_ref[...] = smooth
+
+            @pl.when(slot >= 0)
+            def _():
+                blurred, center = got[...], ext[phase, mid_r, mid_c]
+                spread(slot, center * center, blurred * blurred + center * smooth_ref[...])
+
+        @pl.when(which == 1)
+        def _():
+            @pl.when(slot < 0)
+            def _():
+                residual_ref[...] = right_ref[...] - (got[...] + smooth_ref[...])
+
+            @pl.when(slot >= 0)
+            def _():
+                update(slot)
+
+            @pl.when(phase < phases - 1)
+            def _():
+                put(phase + 1, residual_ref[...])
+
+            @pl.when(slot >= 0)
+            def _():
+                all_slots(slot).wait_send()
+
         finish(phase)
-    for slot in range(ITERS):
-        all_slots(slot).wait_send()
+        return carry
+
+    lax.fori_loop(0, phases, advance, 0)
 
 
 def on_device(n_row, n_col, right_side, initial_guess, kernel):
@@ -314,8 +339,14 @@
         out_specs=(vmem, vmem),
         scratch_shapes=[
             pltpu.VMEM((phases, tall, cols + 2 * EDGE_COLS), jnp.float32),
-            pltpu.VMEM((2, 2 * rows, shifts * rows), jnp.bfloat16),
-            pltpu.VMEM((2, 2 * rows, shifts * 2 * EDGE_ROWS), jnp.bfloat16),
+            pltpu.VMEM((2, LANES, LANES), jnp.float32),
+            pltpu.VMEM((2, shifts * rows // LANES, 2 * rows, LANES), jnp.bfloat16),
+            pltpu.VMEM((2, shifts * 2 * EDGE_ROWS // LANES, 2 * rows, LANES), jnp.bfloat16),
+            pltpu.VMEM((rows, cols), jnp.float32),
+            pltpu.VMEM((rows, cols), jnp.float32),
+            pltpu.VMEM((rows, cols), jnp.float32),
+            pltpu.VMEM((rows, cols), jnp.float32),
+            pltpu.VMEM((8, LANES), jnp.float32),
             pltpu.VMEM((ITERS, count, 1, 128), jnp.float32),
             pltpu.SemaphoreType.DMA((phases, len(DIRECTIONS))),
             pltpu.SemaphoreType.DMA((phases, len(DIRECTIONS))),

time: 53.5 us -> 51.5 us (0.963)
  Pallas kernels: 50.5 us -> 48.5 us
    pallas_call x1, Pallas kernels: 50.5 us -> 48.5 us  [on_device(): pl.pallas_call(functools.partial(body, n_row, n_col), out_shape=(shape, s...]
where the time goes in v3:
time: 51.5 us; the launch traced here: 51.3 us
  Pallas kernels  48.5 us (94%)
  local copies, waits for them, and re-layouts  2.14 us (4%)
  between operations  0.65 us (1%)
    pallas_call x1, Pallas kernels, on_device(): pl.pallas_call(functools.partial(body, n_row, n_col), out_shape=(shape, s...  48.5 us
    unnamed x4, local copies, waits for them, and re-layouts  2.14 us

profile of v3, /device:TPU:0, one launch (start us, length us, event | category | flops | bytes accessed | tf_op | source)
XLA Modules:
  0.0 51.3 jit_solution(3740846913071587024)
XLA Ops:
  0.6 48.5 %shard_map.50 = (f32[64,256]{1,0:T(8,128)}, f32[64,256]{1,0:T(8,128)}) custom-call(f32[64,256]{1,0:T(8,128)} %right_ref.1, f32[64,256]{1,0:T(8,128)} %guess_ref.1, f32[31,31]{1,0:T(8,128)} %kernel_ref.1), custom_call_target="tpu_custom_call" | custom-call | tf_op jit(solution)/shard_map/pallas_call | solution.py:335
  49.2 0.0 copy-start
  49.2 1.5 %copy.7 = f32[64,256]{1,0:T(8,128)} copy(f32[64,256]{1,0:T(8,128)} %get-tuple-element.4) | data formatting | bytes 131072
  50.7 0.0 copy-done
  50.7 0.6 %copy.8 = f32[64,256]{1,0:T(8,128)} copy(f32[64,256]{1,0:T(8,128)S(1)} %copy-done) | data formatting | bytes 131072
Async XLA Ops:
  49.2 1.5 %copy-start = (f32[64,256]{1,0:T(8,128)S(1)}, f32[64,256]{1,0:T(8,128)}, u32[]{:S(2)}) copy-start(f32[64,256]{1,0:T(8,128)} %get-tuple-element.5) | copy-start | bytes 196612
